TPU v7x, 32 devices: a whole 2x2x4 slice. The times are simulated.
32 devices in a mesh: dp: 4 (over x, y), tp: 8 (over z, core).
Axes of the slice: x: 2, y: 2, z: 4, core: 2. Of those that a mesh axis runs over, the one named last changes fastest.
Arguments:
- x: bfloat16 [8192, 5120], P('dp'), parts along dimension 0
- w_gate: bfloat16 [5120, 32768], P(None, 'tp')
- w_up: bfloat16 [5120, 32768], P(None, 'tp')
- w_down: bfloat16 [32768, 5120], P('tp')
Outputs:
- output: bfloat16 [8192, 5120], P('dp'), parts along dimension 0
There are 4 independent parts. A program takes and returns all parts, laid end to end along the dimension named above; an argument that names none is the same for every part.
All inputs are finite; a program needn't handle non-finite values.
Results may differ from a plain program's by a relative error of at most 0.016.
Values are sent between devices in bfloat16 or wider.
A program may use at most 2 GiB of HBM per device.

v0:
```python
import jax
import jax.numpy as jnp
from jax import lax
from jax.sharding import PartitionSpec as P


def solution(mesh):
    def step(x, w_gate, w_up, w_down):
        gate = jnp.dot(x, w_gate, preferred_element_type=jnp.float32)
        up = jnp.dot(x, w_up, preferred_element_type=jnp.float32)
        hidden = (jax.nn.silu(gate) * up).astype(jnp.bfloat16)
        term = jnp.dot(hidden, w_down, preferred_element_type=jnp.float32).astype(jnp.bfloat16)
        return lax.psum(term, "tp")

    return jax.shard_map(
        step,
        mesh=mesh,
        in_specs=(P("dp", None), P(None, "tp"), P(None, "tp"), P("tp", None)),
        out_specs=P("dp", None),
        check_vma=False,
    )
```

profile of v0, /device:TPU:0, one launch (start us, length us, event | category | flops | bytes accessed | tf_op | source)
XLA Modules:
  0.0 743.1 jit_solution(13404807575105607876)
XLA Ops:
  6.5 0.0 all-reduce.2.cloned.1.call-start
  6.5 96.8 %fusion = f32[2048,4096]{1,0:T(8,128)} fusion(bf16[2048,5120]{1,0:T(8,128)(2,1)} %param.4, bf16[5120,4096]{1,0:T(8,128)(2,1)} %param.5), kind=kOutput, calls=%fused_computation.2 | convolution fusion | flops 85899345920 | bytes 96468992 | tf_op jit(solution)/shard_map/dot_general | solution.py:9
  103.3 105.4 %multiply_convert_fusion = bf16[2048,4096]{1,0:T(8,128)(2,1)} fusion(f32[2048,4096]{1,0:T(8,128)} %fusion, bf16[2048,5120]{1,0:T(8,128)(2,1)} %param.4, bf16[5120,4096]{1,0:T(8,128)(2,1)} %param.6), kind=kOutput, calls=%fused_computation | convolution fusion | flops 85949677568 | bytes 113246208 | tf_op jit(solution)/shard_map/dot_general | solution.py:10
  208.7 95.9 %convolution_convert_fusion = bf16[2048,5120]{1,0:T(8,128)(2,1)} fusion(bf16[2048,4096]{1,0:T(8,128)(2,1)} %multiply_convert_fusion, bf16[4096,5120]{1,0:T(8,128)(2,1)} %param.7), kind=kOutput, calls=%fused_computation.1 | convolution fusion | flops 85909831680 | bytes 79691776 | tf_op jit(solution)/shard_map/dot_general | solution.py:12
  304.6 0.0 all-reduce.2.cloned.1.call-update
  304.6 414.4 %all-reduce.2.cloned.1.call-done = bf16[2048,5120]{1,0:T(8,128)(2,1)} async-done(((bf16[2048,5120]{1,0:T(8,128)(2,1)}), bf16[2048,5120]{1,0:T(8,128)(2,1)}) %all-reduce.2.cloned.1.call-update) | async-done | bytes 20971536 | tf_op jit(solution)/shard_map/psum | solution.py:13
  719.0 17.3 %copy.6 = bf16[2048,5120]{1,0:T(8,128)(2,1)} copy(bf16[2048,5120]{1,0:T(8,128)(2,1)} %all-reduce.2.cloned.1.call-done) | data formatting | bytes 41943040
Async XLA Ops:
  6.5 712.4 %all-reduce.2.cloned.1.call-start = ((), (), s32[]{:S(2)}) async-start(), calls=%async_computation | async-start | bytes 41943040 | tf_op jit(solution)/shard_map/psum | solution.py:13
Sparse Core Ops, SparseCore 0:
  304.7 414.2 all-reduce.1
where the time goes:
time: 743 us
  waiting for transfers between devices  414 us (56%)
  matrix products  298 us (40%)
  local copies, waits for them, and re-layouts  17.3 us (2%)
  between operations  13.4 us (2%)
    psum x1, waiting for transfers between devices, step(): return lax.psum(term, 'tp')  414 us
    dot_general x1, matrix products, step(): up = jnp.dot(x, w_up, preferred_element_type=jnp.float32)  105 us
    dot_general x1, matrix products, step(): gate = jnp.dot(x, w_gate, preferred_element_type=jnp.float32)  96.8 us
    dot_general x1, matrix products, step(): jnp.dot(hidden, w_down, preferred_element_type=jnp.float32)  95.9 us
    unnamed x1, local copies, waits for them, and re-layouts  17.3 us
  transfers between devices with their start and end apart: 1, of which 1 were waited for; matrix products, arithmetic and copies ran while one was open for 0% of the time, Pallas kernels for 0%

commit v1 on v0

v1 whole, which is shorter than its diff:
```python
import jax
import jax.numpy as jnp
from jax import lax
from jax.experimental import pallas as pl
from jax.experimental.pallas import tpu as pltpu
from jax.sharding import PartitionSpec as P

MESH = pl.DeviceIdType.MESH
BF, F32 = jnp.bfloat16, jnp.float32

CH = 512
TG = 256
TD = 512
HALF = 128

L1, L2, L3, L4, L5 = 2, 4, 6, 8, 10
NS = 8
NK = 7
NG = 3
NX = 4


def kernel(x, wg, wu, wd, y, xb, gb, ub, db, hid, keep, xs, xr, es, er, ms, mr, ys,
           xsem, gsem, usem, dsem, xs_s, xr_s, es_s, er_s, ms_s, mr_s, ys_s, yo_s, ye_s, yp_s, fw_s):
    rows, width = x.shape
    ff = wg.shape[1]
    nch, ng, nd = rows // CH, ff // TG, width // TD
    npairs = nch * nd
    t_idx = lax.axis_index("tp")
    z, c = t_idx // 2, t_idx % 2
    side = z // 2
    mid = (z == 1) | (z == 2)
    end = jnp.logical_not(mid)
    partner = {"tp": z * 2 + 1 - c}
    inner = {"tp": (1 + side) * 2 + c}
    outer = {"tp": 3 * side * 2 + c}
    across = {"tp": (2 - side) * 2 + c}

    def remote(src, dst, ssem, rsem, dev):
        return pltpu.make_async_remote_copy(
            src_ref=src, dst_ref=dst, send_sem=ssem, recv_sem=rsem, device_id=dev, device_id_type=MESH
        )

    def sl(q, n):
        return lax.rem(q + 8 * n, n)

    def x_copy(ch):
        b = lax.rem(ch, 2)
        return pltpu.make_async_copy(x.at[pl.ds(ch * CH, CH), :], xb.at[b], xsem.at[b])

    def g_copies(g):
        cols = pl.ds(pl.multiple_of(lax.rem(g, ng) * TG, TG), TG)
        s = lax.rem(g, NG)
        return (
            pltpu.make_async_copy(wg.at[:, cols], gb.at[s], gsem.at[s]),
            pltpu.make_async_copy(wu.at[:, cols], ub.at[s], usem.at[s]),
        )

    def d_copy(d):
        cols = pl.ds(pl.multiple_of(lax.rem(d, nd) * TD, TD), TD)
        s = lax.rem(d, 2)
        return pltpu.make_async_copy(wd.at[:, cols], db.at[s], dsem.at[s])

    def g_top(g):
        for cp in g_copies(g):
            cp.wait()

        @pl.when(g + NG - 1 < nch * ng)
        def _():
            for cp in g_copies(g + NG - 1):
                cp.start()

    def d_top(d):
        d_copy(d).wait()

        @pl.when(d + 1 < npairs)
        def _():
            d_copy(d + 1).start()

    def g_body(g):
        s, par = lax.rem(g, NG), lax.rem(g // ng, 2)
        gate = jnp.dot(xb[par], gb[s], preferred_element_type=F32)
        up = jnp.dot(xb[par], ub[s], preferred_element_type=F32)
        cols = pl.ds(pl.multiple_of(lax.rem(g, ng) * TG, TG), TG)
        hid[par, :, cols] = (gate * jax.nn.sigmoid(gate) * up).astype(BF)

    def d_body(d):
        part = jnp.dot(hid[lax.rem(d // nd, 2)], db[lax.rem(d, 2)], preferred_element_type=F32)
        s, sx = lax.rem(d, NK), lax.rem(d, NX)
        for u in range(2):
            a = part[2 * u * HALF : (2 * u + 1) * HALF]
            b = part[(2 * u + 1) * HALF : (2 * u + 2) * HALF]
            keep[s, u] = jnp.where(c == 0, a, b)
            xs[sx, u] = jnp.where(c == 0, b, a).astype(BF)

    def place(q, piece, n=1):
        row = (q // nd) * CH + piece * 2 * HALF + c * HALF
        return y.at[
            pl.ds(pl.multiple_of(row, HALF), n * HALF),
            pl.ds(pl.multiple_of(lax.rem(q, nd) * TD, TD), TD),
        ]

    def swap(q):
        sx, s = sl(q, NX), sl(q, NS)
        return remote(xs.at[sx], xr.at[s], xs_s.at[sx], xr_s.at[s], partner)

    def inward(q):
        sx, s = sl(q, NX), sl(q, NS)
        return remote(es.at[sx], er.at[s], es_s.at[sx], er_s.at[s], inner)

    def cross(q):
        sx, s = sl(q, NX), sl(q, NS)
        return remote(ms.at[sx], mr.at[s], ms_s.at[sx], mr_s.at[s], across)

    def finals(q):
        sx = sl(q, NX)
        dst = place(q, side)
        return (
            remote(ys.at[sx], dst, ys_s.at[sx, 0], yo_s.at[q], across),
            remote(ys.at[sx], dst, ys_s.at[sx, 1], ye_s.at[q, 0], outer),
            remote(ys.at[sx], dst, ys_s.at[sx, 2], yp_s.at[q, 0], partner),
            pltpu.make_async_copy(ys.at[sx], dst, ys_s.at[sx, 3]),
        )

    def sent_finals(q):
        cps = finals(q)
        for cp in cps[:3]:
            cp.wait_send()
        cps[3].wait()

    def from_across(q):
        ref = place(q, 1 - side)
        return remote(ref, ref, fw_s.at[0], yo_s.at[q], across)

    def mid_forward(q):
        ref = place(q, 1 - side)
        return (
            remote(ref, ref, fw_s.at[0], ye_s.at[q, 1], outer),
            remote(ref, ref, fw_s.at[1], yp_s.at[q, 1], partner),
        )

    def end_forward(q):
        return [
            remote(place(q, p), place(q, p), fw_s.at[k], yp_s.at[q, k], partner)
            for k, p in ((0, side), (1, 1 - side))
        ]

    def end_arrivals(q):
        return [
            remote(place(q, p), place(q, p), fw_s.at[k], ye_s.at[q, k], inner)
            for k, p in ((0, side), (1, 1 - side))
        ]

    def held(q):
        return jnp.where(q < 0, NS, lax.rem(q + NS, NS))

    def live(q):
        return (q >= 0) & (q < npairs)

    def arrive(t):
        @pl.when(live(t - L4) & mid)
        def _():
            from_across(t - L4).wait_recv()
            for cp in mid_forward(t - L4):
                cp.start()

        @pl.when(live(t - L5) & end)
        def _():
            for cp in end_arrivals(t - L5):
                cp.wait_recv()
            for cp in end_forward(t - L5):
                cp.start()

        @pl.when(live(t - NX))
        def _():
            swap(t - NX).wait_send()

        @pl.when(live(t - L1 - NX) & end)
        def _():
            inward(t - L1 - NX).wait_send()

        @pl.when(live(t - L2 - NX) & mid)
        def _():
            cross(t - L2 - NX).wait_send()

        @pl.when(live(t - L3 - NX) & mid)
        def _():
            sent_finals(t - L3 - NX)

        @pl.when(live(t - L1))
        def _():
            swap(t - L1).wait_recv()

        @pl.when(live(t - L2) & mid)
        def _():
            inward(t - L2).wait_recv()

        @pl.when(live(t - L3) & mid)
        def _():
            cross(t - L3).wait_recv()

    def leave(t):
        swap(t).start()

        @pl.when(live(t - L1) & end)
        def _():
            inward(t - L1).start()

        @pl.when(live(t - L2) & mid)
        def _():
            cross(t - L2).start()

        @pl.when(live(t - L3) & mid)
        def _():
            for cp in finals(t - L3):
                cp.start()

    def stage1(q):
        s = sl(q, NS)
        es[sl(q, NX)] = (keep[sl(q, NK)] + xr[s].astype(F32)).astype(BF)

    def stage2(q):
        s = sl(q, NS)
        e, k = held(q), sl(q, NK)
        own = keep[k, side] + xr[s, side].astype(F32) + er[e, side].astype(F32)
        far = keep[k, 1 - side] + xr[s, 1 - side].astype(F32) + er[e, 1 - side].astype(F32)
        keep[k, side] = own
        ms[sl(q, NX)] = far.astype(BF)

    def stage3(q):
        ys[sl(q, NX)] = (keep[sl(q, NK), side] + mr[held(q)].astype(F32)).astype(BF)

    def stages(t):
        stage3(t - L3)
        stage2(t - L2)
        stage1(t - L1)

    x_copy(0).start()
    for k in range(NG - 1):
        for cp in g_copies(k):
            cp.start()
    d_copy(0).start()
    barrier = pltpu.get_barrier_semaphore()
    pl.semaphore_signal(barrier, inc=1, device_id=partner, device_id_type=MESH)

    @pl.when(end)
    def _():
        pl.semaphore_signal(barrier, inc=1, device_id=inner, device_id_type=MESH)

    @pl.when(mid)
    def _():
        pl.semaphore_signal(barrier, inc=1, device_id=outer, device_id_type=MESH)
        pl.semaphore_signal(barrier, inc=1, device_id=across, device_id_type=MESH)

    @pl.when(end)
    def _():
        pl.semaphore_wait(barrier, 2)

    @pl.when(mid)
    def _():
        pl.semaphore_wait(barrier, 3)

    x_copy(0).wait()
    x_copy(1).start()

    def first(i, _):
        g_top(i)
        g_body(i)
        return 0

    lax.fori_loop(0, ng, first, 0)

    gh, dh = ng // 2, nd // 2

    def half_chunk(h, _):
        ch = h // 2 + 1

        @pl.when(h % 2 == 0)
        def _():
            x_copy(ch).wait()

            @pl.when(ch + 1 < nch)
            def _():
                x_copy(ch + 1).start()

        def tick(i, _):
            o = (gh * i + dh - 1) // dh
            g, d = ng + h * gh + o, h * dh + i
            arrive(d)
            g_top(g)
            d_top(d)
            g_body(g)
            d_body(d)
            stages(d)
            leave(d)

            @pl.when((gh * (i + 1) + dh - 1) // dh - o == 2)
            def _():
                g_top(g + 1)
                g_body(g + 1)

            return 0

        lax.fori_loop(0, dh, tick, 0)
        return 0

    lax.fori_loop(0, 2 * (nch - 1), half_chunk, 0)

    t0 = (nch - 1) * nd

    def upto(i, done, goal, by):
        return jnp.minimum(jnp.minimum(t0 - done + by * i, t0 - goal + i), npairs)

    def ranged(i, done, goal, body):
        lax.fori_loop(upto(i, done, goal, 2), upto(i + 1, done, goal, 2), body, 0)

    def tail(i, _):
        d = t0 + i

        @pl.when(d < npairs)
        def _():
            d_top(d)
            swap(d - NX).wait_send()
            d_body(d)
            swap(d).start()

        def one(q, _):
            swap(q).wait_recv()

            @pl.when(end)
            def _():
                inward(q - NX).wait_send()
                stage1(q)
                inward(q).start()

            return 0

        def two(q, _):
            inward(q).wait_recv()
            cross(q - NX).wait_send()
            stage2(q)
            cross(q).start()
            return 0

        def three(q, _):
            cross(q).wait_recv()
            sent_finals(q - NX)
            stage3(q)
            for cp in finals(q):
                cp.start()
            return 0

        def four(q, _):
            from_across(q).wait_recv()
            for cp in mid_forward(q):
                cp.start()
            return 0

        def five(q, _):
            for cp in end_arrivals(q):
                cp.wait_recv()
            for cp in end_forward(q):
                cp.start()
            return 0

        @pl.when(end)
        def _():
            ranged(i, L5, L2 + 6, five)

        ranged(i, L1, 1, one)

        @pl.when(mid)
        def _():
            ranged(i, L2, L2, two)
            ranged(i, L3, L2 + 1, three)
            ranged(i, L4, L2 + 3, four)

        return 0

    lax.fori_loop(0, nd + L2 + 6, tail, 0)

    for q in range(npairs - NX, npairs):
        swap(q).wait_send()

        @pl.when(end)
        def _():
            inward(q).wait_send()

        @pl.when(mid)
        def _():
            cross(q).wait_send()
            sent_finals(q)

    def arrivals(q, _):
        for k in range(2):
            remote(place(q, 0), place(q, 0), fw_s.at[0], yp_s.at[q, k], partner).wait_recv()
        return 0

    lax.fori_loop(0, npairs, arrivals, 0)
    for k in range(2):
        ref = y.at[pl.ds(0, npairs * HALF * TD // width), :]
        remote(ref, ref, fw_s.at[k], yp_s.at[0, 0], partner).wait_send()


def block(x, w_gate, w_up, w_down):
    rows, width = x.shape
    ff = w_gate.shape[1]
    npairs = (rows // CH) * (width // TD)
    vm = pltpu.VMEM
    dma = pltpu.SemaphoreType.DMA
    return pl.pallas_call(
        kernel,
        out_shape=jax.ShapeDtypeStruct((rows, width), BF),
        in_specs=[pl.BlockSpec(memory_space=pl.ANY)] * 4,
        out_specs=pl.BlockSpec(memory_space=pl.ANY),
        scratch_shapes=[
            vm((2, CH, width), BF),
            vm((NG, width, TG), BF),
            vm((NG, width, TG), BF),
            vm((2, ff, TD), BF),
            vm((2, CH, ff), BF),
            vm((NK, 2, HALF, TD), F32),
            vm((NX, 2, HALF, TD), BF),
            vm((NS, 2, HALF, TD), BF),
            vm((NX, 2, HALF, TD), BF),
            vm((NS + 1, 2, HALF, TD), BF),
            vm((NX, HALF, TD), BF),
            vm((NS + 1, HALF, TD), BF),
            vm((NX, HALF, TD), BF),
            dma((2,)),
            dma((NG,)),
            dma((NG,)),
            dma((2,)),
            dma((NX,)),
            dma((NS,)),
            dma((NX,)),
            dma((NS,)),
            dma((NX,)),
            dma((NS,)),
            dma((NX, 4)),
            dma((npairs,)),
            dma((npairs, 2)),
            dma((npairs, 2)),
            dma((2,)),
        ],
        compiler_params=pltpu.CompilerParams(
            collective_id=0, has_side_effects=True, vmem_limit_bytes=67043328
        ),
    )(x, w_gate, w_up, w_down)


def solution(mesh):
    return jax.shard_map(
        block,
        mesh=mesh,
        in_specs=(P("dp", None), P(None, "tp"), P(None, "tp"), P("tp", None)),
        out_specs=P("dp", None),
        check_vma=False,
    )
```

time: 743 us -> 395 us (0.53)
  waiting for transfers between devices: 414 us -> 0 us
  Pallas kernels: 0 us -> 378 us
  matrix products: 298 us -> 0 us
  between operations: 13.4 us -> 0.01 us
    psum x1 -> x0, waiting for transfers between devices: 414 us -> none  [step(): return lax.psum(term, 'tp')]
    pallas_call x0 -> x1, Pallas kernels: none -> 378 us  [block(): pl.pallas_call(kernel, out_shape=jax.ShapeDtypeStruct((rows, width), BF),...]
    dot_general x3 -> x0, matrix products: 298 us -> none  [the longest x1 105 us: step(): up = jnp.dot(x, w_up, preferred_element_type=jnp.float32)]
  transfers between devices with their start and end apart: 1 -> 0, of which waited for: 1 -> 0; matrix products, arithmetic and copies ran while one was open for 0% -> 0% of each run, Pallas kernels for 0% -> 0%
where the time goes in v1:
time: 395 us
  Pallas kernels  378 us (96%)
  local copies, waits for them, and re-layouts  17.3 us (4%)
    pallas_call x1, Pallas kernels, block(): pl.pallas_call(kernel, out_shape=jax.ShapeDtypeStruct((rows, width), BF),...  378 us
    unnamed x1, local copies, waits for them, and re-layouts  17.3 us

profile of v1, /device:TPU:0, one launch (start us, length us, event | category | flops | bytes accessed | tf_op | source)
XLA Modules:
  0.0 395.2 jit_solution(1131665712889534163)
XLA Ops:
  0.0 377.9 %shard_map.46 = bf16[2048,5120]{1,0:T(8,128)(2,1)} custom-call(bf16[2048,5120]{1,0:T(8,128)(2,1)} %x.1, bf16[5120,4096]{1,0:T(8,128)(2,1)} %wg.1, bf16[5120,4096]{1,0:T(8,128)(2,1)} %wu.1, bf16[4096,5120]{1,0:T(8,128)(2,1)} %wd.1), custom_call_target="tpu_custom_call" | custom-call | tf_op jit(solution)/shard_map/pallas_call | solution.py:411
  377.9 17.3 %copy.6 = bf16[2048,5120]{1,0:T(8,128)(2,1)} copy(bf16[2048,5120]{1,0:T(8,128)(2,1)} %shard_map.46) | data formatting | bytes 41943040
